TPU v7x, 32 devices: a whole 2x2x4 slice. The times are simulated.
32 devices in a mesh: dp: 32 (over z, y, x, core), tensor: 1.
Axes of the slice: x: 2, y: 2, z: 4, core: 2. Of those that a mesh axis runs over, the one named last changes fastest.
Arguments:
- activations: bfloat16 [384, 8192], P('dp', 'tensor'), may hold values from -400 to 400, as said below
- weight: bfloat16 [8192, 28672], P('dp', 'tensor'), may hold values from -0.0625 to 0.0625
Outputs:
- channel_mean: float32 [8192], P('dp')
- column_errors: float32 [4, 28672], P(None, ('tensor', 'dp'))
- errors: float32 [4], replicated
Inputs may be any that keep to these rules, and one draw needn't show every extreme that they name: activations and weight are finite real values within the ranges stated above.
All inputs are finite; a program needn't handle non-finite values.
Results may differ from a plain program's by a relative error of at most 0.0012.
The roundings to bfloat16 on the way count: a program that leaves them out, or rounds other values in their place, can miss the bound.
Values may be sent and summed in bfloat16 or wider, within the bound.
A program may use at most 128 MiB of HBM per device.

v0:
```python
import math
import jax
import jax.numpy as jnp
from jax import lax
from jax.sharding import PartitionSpec as P

D = 8192
F = 28672
GROUP = 128
GRID = 4


def soft_round(values):
    return values - jnp.sin(2.0 * math.pi * values) / (2.0 * math.pi)


def scale_table(channel_mean):
    ratios = jnp.arange(GRID, dtype=jnp.float32) / GRID
    raw = jnp.exp(ratios[:, None] * jnp.log(channel_mean)[None, :])
    top = jnp.max(raw, axis=1, keepdims=True)
    bottom = jnp.min(raw, axis=1, keepdims=True)
    return raw / jnp.sqrt(top * bottom)


def on_device(activations, weight):
    widened = lax.all_gather(activations, "tensor", axis=1, tiled=True)
    gathered = lax.all_gather(widened, "dp", axis=0, tiled=True)
    columns = lax.all_to_all(weight, "dp", split_axis=1, concat_axis=0, tiled=True)
    width = columns.shape[1]
    token_count = gathered.shape[0]
    channel_mean = jnp.sum(jnp.abs(gathered), axis=0, dtype=jnp.float32) / token_count + 1e-06
    scales = scale_table(channel_mean)
    base_out = jnp.dot(gathered, columns, preferred_element_type=jnp.float32)
    weight_float = columns.astype(jnp.float32)

    def local_error(factor):
        scaled = weight_float * factor[:, None]
        grouped = scaled.reshape(D // GROUP, GROUP, width)
        quant_step = (jnp.max(jnp.abs(grouped), axis=1, keepdims=True) + 1e-06) / 7.0
        levels = soft_round(grouped / quant_step)
        dequant = ((levels * quant_step).reshape(D, width) / factor[:, None]).astype(jnp.bfloat16)
        quant_out = jnp.dot(gathered, dequant, preferred_element_type=jnp.float32)
        residue = quant_out - base_out
        return jnp.sum(residue * residue, axis=0)

    column_sums = lax.map(local_error, scales)
    totals = lax.psum(jnp.sum(column_sums, axis=1), ("dp", "tensor"))
    errors = totals / (token_count * F)
    column_errors = column_sums / token_count
    rows = D // lax.axis_size("dp")
    own_mean = lax.dynamic_slice_in_dim(channel_mean, lax.axis_index("dp") * rows, rows)
    return (own_mean, column_errors, errors)


def solution(mesh):
    placed = (P("dp", "tensor"), P("dp", "tensor"))
    return jax.shard_map(
        on_device,
        mesh=mesh,
        in_specs=placed,
        out_specs=(P("dp"), P(None, ("tensor", "dp")), P()),
        check_vma=False,
    )
```

profile of v0, /device:TPU:10, one launch (start us, length us, event | category | flops | bytes accessed | tf_op | source)
XLA Modules:
  0.0 1007.1 jit_solution(17672235524525206103)
XLA Ops:
  7.2 14.7 %copy.10 = bf16[32,32,8,896]{3,2,0,1:T(8,128)(2,1)} copy(bf16[32,32,8,896]{3,2,1,0:T(8,128)(2,1)} %bitcast.49) | data formatting | bytes 29360128 | tf_op jit(solution)/shard_map/all_to_all | solution.py:28
  21.9 6.1 all-to-all-start
  28.0 0.7 all-gather.3.cloned.1.call-update
  28.7 192.3 %all-gather.3.cloned.1.call-done = bf16[32,12,8192]{2,1,0:T(8,128)(2,1)} async-done(((bf16[1,12,8192]{2,1,0:T(8,128)(2,1)}), bf16[32,12,8192]{2,1,0:T(8,128)(2,1)}) %all-gather.3.cloned.1.call-update) | async-done | bytes 6291472 | tf_op jit(solution)/shard_map/all_gather | solution.py:27
  221.0 8.8 reshape.50
  229.8 4.2 convert_reduce_fusion
  233.9 0.6 dynamic_slice.7
  234.6 0.3 fusion.6
  234.9 0.1 fusion.5
  235.0 147.9 %all-to-all-done = bf16[256,32,896]{2,0,1:T(8,128)(2,1)} async-done(((bf16[256,32,896]{2,0,1:T(8,128)(2,1)}), bf16[256,32,896]{2,0,1:T(8,128)(2,1)}, u32[]{:S(2)}, u32[]{:S(2)}) %all-to-all-start) | async-done | bytes 14680096 | tf_op jit(solution)/shard_map/all_to_all | solution.py:28
  382.9 12.0 %fusion.10 = f32[384,896]{1,0:T(8,128)} fusion(bf16[384,8192]{1,0:T(8,128)(2,1)} %reshape.50, bf16[8192,896]{1,0:T(8,128)(2,1)} %bitcast.7), kind=kOutput, calls=%fused_computation.25 | convolution fusion | flops 5637144576 | bytes 22347776 | tf_op jit(solution)/shard_map/dot_general | solution.py:33
  394.9 16.6 %bitcast_convert_fusion = f32[8192,896]{1,0:T(8,128)} fusion(bf16[256,32,896]{2,0,1:T(8,128)(2,1)} %all-to-all-done), kind=kLoop, calls=%fused_computation.22 | loop fusion | flops 7340032 | bytes 44040192 | tf_op jit(solution)/shard_map/convert_element_type | solution.py:34
  411.4 541.8 %while.10 = (s32[]{:T(128)}, f32[4,896]{1,0:T(4,128)S(1)}, f32[4,8192]{1,0:T(4,128)S(1)}, f32[8192,896]{1,0:T(8,128)}, bf16[384,8192]{1,0:T(8,128)(2,1)}, /*index=5*/f32[384,896]{1,0:T(8,128)}, s32[]{:T(128)}, s32[]{:T(128)}) while((s32[]{:T(128)}, f32[4,896]{1,0:T(4,128)S(1)}, f32[4,8192]{1,0:T(4,128)S(1)}, f32[8192,896]{1,0:T(8,128)}, ...), condition=%wide.region_6.7_spmd, body=%wide.region_3.6_spmd.sunk | while | flops 5718973440 | bytes 214255232 | solution.py:46
  411.5 12.5 %abs_reduce_fusion.2 = f32[64,896]{1,0:T(8,128)S(1)} fusion(f32[64,128]{1,0:T(8,128)S(1)} %bitcast.50, f32[8192,896]{1,0:T(8,128)} %get-tuple-element.110), kind=kLoop, calls=%fused_computation.4.clone.1 | loop fusion | flops 21962752 | bytes 29622272 | tf_op jit(solution)/shard_map/while/body/eval_jaxpr/reduce_max | solution.py:39
  424.0 5.2 copy-done
  429.2 108.3 %fusion.21 = bf16[8192,896]{1,0:T(8,128)(2,1)S(1)} fusion(f32[8192,896]{1,0:T(8,128)S(1)} %copy-done, f32[64,896]{1,0:T(8,128)S(1)} %add_multiply_fusion.2, f32[8192]{0:T(1024)S(1)} %bitcast.51), kind=kLoop, calls=%fused_computation.3.clone.1 | loop fusion | flops 58720256 | bytes 44302336 | tf_op jit(solution)/shard_map/while/body/eval_jaxpr/convert_element_type | solution.py:41
  537.5 9.3 fusion.22
  546.9 12.5 %abs_reduce_fusion.2 = f32[64,896]{1,0:T(8,128)S(1)} fusion(f32[64,128]{1,0:T(8,128)S(1)} %bitcast.50, f32[8192,896]{1,0:T(8,128)} %get-tuple-element.110), kind=kLoop, calls=%fused_computation.4.clone.1 | loop fusion | flops 21962752 | bytes 29622272 | tf_op jit(solution)/shard_map/while/body/eval_jaxpr/reduce_max | solution.py:39
  559.4 5.2 copy-done
  564.7 108.3 %fusion.21 = bf16[8192,896]{1,0:T(8,128)(2,1)S(1)} fusion(f32[8192,896]{1,0:T(8,128)S(1)} %copy-done, f32[64,896]{1,0:T(8,128)S(1)} %add_multiply_fusion.2, f32[8192]{0:T(1024)S(1)} %bitcast.51), kind=kLoop, calls=%fused_computation.3.clone.1 | loop fusion | flops 58720256 | bytes 44302336 | tf_op jit(solution)/shard_map/while/body/eval_jaxpr/convert_element_type | solution.py:41
  673.0 9.2 fusion.22
  682.4 12.5 %abs_reduce_fusion.2 = f32[64,896]{1,0:T(8,128)S(1)} fusion(f32[64,128]{1,0:T(8,128)S(1)} %bitcast.50, f32[8192,896]{1,0:T(8,128)} %get-tuple-element.110), kind=kLoop, calls=%fused_computation.4.clone.1 | loop fusion | flops 21962752 | bytes 29622272 | tf_op jit(solution)/shard_map/while/body/eval_jaxpr/reduce_max | solution.py:39
  694.9 5.2 copy-done
  700.1 108.3 %fusion.21 = bf16[8192,896]{1,0:T(8,128)(2,1)S(1)} fusion(f32[8192,896]{1,0:T(8,128)S(1)} %copy-done, f32[64,896]{1,0:T(8,128)S(1)} %add_multiply_fusion.2, f32[8192]{0:T(1024)S(1)} %bitcast.51), kind=kLoop, calls=%fused_computation.3.clone.1 | loop fusion | flops 58720256 | bytes 44302336 | tf_op jit(solution)/shard_map/while/body/eval_jaxpr/convert_element_type | solution.py:41
  808.4 9.3 fusion.22
  817.8 12.5 %abs_reduce_fusion.2 = f32[64,896]{1,0:T(8,128)S(1)} fusion(f32[64,128]{1,0:T(8,128)S(1)} %bitcast.50, f32[8192,896]{1,0:T(8,128)} %get-tuple-element.110), kind=kLoop, calls=%fused_computation.4.clone.1 | loop fusion | flops 21962752 | bytes 29622272 | tf_op jit(solution)/shard_map/while/body/eval_jaxpr/reduce_max | solution.py:39
  830.3 5.2 copy-done
  835.6 108.3 %fusion.21 = bf16[8192,896]{1,0:T(8,128)(2,1)S(1)} fusion(f32[8192,896]{1,0:T(8,128)S(1)} %copy-done, f32[64,896]{1,0:T(8,128)S(1)} %add_multiply_fusion.2, f32[8192]{0:T(1024)S(1)} %bitcast.51), kind=kLoop, calls=%fused_computation.3.clone.1 | loop fusion | flops 58720256 | bytes 44302336 | tf_op jit(solution)/shard_map/while/body/eval_jaxpr/convert_element_type | solution.py:41
  943.9 9.3 fusion.22
  953.2 0.7 fusion.9
  954.0 45.8 %psum.7 = f32[4]{0:T(128)S(1)} all-reduce(f32[4]{0:T(128)S(1)} %get-tuple-element.52), channel_id=1, replica_groups=mesh['dp'=32,'tensor'=1] {'dp','tensor'}, use_global_device_ids=true, to_apply=%region_8.9 | all-reduce | flops 4 | bytes 32 | tf_op jit(solution)/shard_map/psum | solution.py:47
  999.8 0.5 broadcast_multiply_fusion.1
  (25 shorter events, 0.6 us)
Async XLA Ops:
  21.9 361.0 %all-to-all-start = ((bf16[256,32,896]{2,0,1:T(8,128)(2,1)}), bf16[256,32,896]{2,0,1:T(8,128)(2,1)}, u32[]{:S(2)}, u32[]{:S(2)}) async-start(bf16[256,32,896]{2,0,1:T(8,128)(2,1)} %bitcast.48), calls=%async_computation | async-start | bytes 29360128 | tf_op jit(solution)/shard_map/all_to_all | solution.py:28
  27.9 193.0 %all-gather.3.cloned.1.call-start = ((), (), s32[]{:S(2)}) async-start(), calls=%async_computation.1 | async-start | bytes 8650752 | tf_op jit(solution)/shard_map/all_gather | solution.py:27
  411.5 17.8 %copy-start = (f32[8192,896]{1,0:T(8,128)S(1)}, f32[8192,896]{1,0:T(8,128)}, u32[]{:S(2)}) copy-start(f32[8192,896]{1,0:T(8,128)} %get-tuple-element.110) | copy-start | bytes 88080384 | tf_op jit(solution)/shard_map/while
  546.9 17.8 %copy-start = (f32[8192,896]{1,0:T(8,128)S(1)}, f32[8192,896]{1,0:T(8,128)}, u32[]{:S(2)}) copy-start(f32[8192,896]{1,0:T(8,128)} %get-tuple-element.110) | copy-start | bytes 88080384 | tf_op jit(solution)/shard_map/while
  682.4 17.8 %copy-start = (f32[8192,896]{1,0:T(8,128)S(1)}, f32[8192,896]{1,0:T(8,128)}, u32[]{:S(2)}) copy-start(f32[8192,896]{1,0:T(8,128)} %get-tuple-element.110) | copy-start | bytes 88080384 | tf_op jit(solution)/shard_map/while
  817.8 17.8 %copy-start = (f32[8192,896]{1,0:T(8,128)S(1)}, f32[8192,896]{1,0:T(8,128)}, u32[]{:S(2)}) copy-start(f32[8192,896]{1,0:T(8,128)} %get-tuple-element.110) | copy-start | bytes 88080384 | tf_op jit(solution)/shard_map/while
Sparse Core Ops, SparseCore 0:
  31.6 189.3 all-gather.2
where the time goes:
time: 1010 us
  other arithmetic  506 us (50%)
  waiting for transfers between devices  341 us (34%)
  matrix products  49 us (5%)
  blocking collectives  45.8 us (5%)
  local copies, waits for them, and re-layouts  45.5 us (5%)
  between operations  14.1 us (1%)
    convert_element_type x4, other arithmetic, local_error(): ((levels * quant_step).reshape(D, width) / factor[:, None]).astype(jnp.bf...  433 us
    all_gather x1, waiting for transfers between devices, on_device(): gathered = lax.all_gather(widened, 'dp', axis=0, tiled=True)  192 us
    all_to_all x1, waiting for transfers between devices, on_device(): lax.all_to_all(weight, 'dp', split_axis=1, concat_axis=0, tiled=True)  148 us
    reduce_max x4, other arithmetic, local_error(): jnp.max(jnp.abs(grouped), axis=1, keepdims=True) + 1e-06  49.8 us
    psum x1, blocking collectives, on_device(): totals = lax.psum(jnp.sum(column_sums, axis=1), ('dp', 'tensor'))  45.8 us
    dot_general x4, matrix products, local_error(): quant_out = jnp.dot(gathered, dequant, preferred_element_type=jnp.float32)  37 us
    while x8, local copies, waits for them, and re-layouts  21 us
  transfers between devices with their start and end apart: 2, of which 2 were waited for; matrix products, arithmetic and copies ran while one was open for 1% of the time, Pallas kernels for 0%

commit v1 on v0

--- a/solution.py
+++ b/solution.py
@@ -8,6 +8,13 @@
 F = 28672
 GROUP = 128
 GRID = 4
+
+
+def stacked_exchange(array, axis, split, join):
+    size = lax.axis_size(axis)
+    pieces = jnp.stack(jnp.split(array, size, axis=split), axis=0)
+    pieces = lax.all_to_all(pieces, axis, split_axis=0, concat_axis=0)
+    return jnp.concatenate(pieces, axis=join)
 
 
 def soft_round(values):
@@ -25,7 +32,7 @@
 def on_device(activations, weight):
     widened = lax.all_gather(activations, "tensor", axis=1, tiled=True)
     gathered = lax.all_gather(widened, "dp", axis=0, tiled=True)
-    columns = lax.all_to_all(weight, "dp", split_axis=1, concat_axis=0, tiled=True)
+    columns = stacked_exchange(weight, "dp", 1, 0)
     width = columns.shape[1]
     token_count = gathered.shape[0]
     channel_mean = jnp.sum(jnp.abs(gathered), axis=0, dtype=jnp.float32) / token_count + 1e-06

time: 1010 us -> 1050 us (1.040)
  local copies, waits for them, and re-layouts: 45.5 us -> 91 us
    unnamed x1 -> x32, local copies, waits for them, and re-layouts: 8.77 us -> 65.6 us
    all_to_all x1 -> x0, local copies, waits for them, and re-layouts: 14.7 us -> none  [on_device(): lax.all_to_all(weight, 'dp', split_axis=1, concat_axis=0, tiled=True)]
    while x8 -> x9, local copies, waits for them, and re-layouts: 21 us -> 22.5 us
where the time goes in v1:
time: 1050 us
  other arithmetic  506 us (48%)
  waiting for transfers between devices  341 us (32%)
  local copies, waits for them, and re-layouts  91 us (9%)
  matrix products  49 us (5%)
  blocking collectives  45.8 us (4%)
  between operations  14.1 us (1%)
    convert_element_type x4, other arithmetic, local_error(): ((levels * quant_step).reshape(D, width) / factor[:, None]).astype(jnp.bf...  433 us
    all_gather x1, waiting for transfers between devices, on_device(): gathered = lax.all_gather(widened, 'dp', axis=0, tiled=True)  192 us
    all_to_all x1, waiting for transfers between devices, stacked_exchange(): pieces = lax.all_to_all(pieces, axis, split_axis=0, concat_axis=0)  148 us
    unnamed x32, local copies, waits for them, and re-layouts  65.6 us
    reduce_max x4, other arithmetic, local_error(): jnp.max(jnp.abs(grouped), axis=1, keepdims=True) + 1e-06  49.8 us
    psum x1, blocking collectives, on_device(): totals = lax.psum(jnp.sum(column_sums, axis=1), ('dp', 'tensor'))  45.8 us
    dot_general x4, matrix products, local_error(): quant_out = jnp.dot(gathered, dequant, preferred_element_type=jnp.float32)  37 us
  transfers between devices with their start and end apart: 2, of which 2 were waited for; matrix products, arithmetic and copies ran while one was open for 1% of the time, Pallas kernels for 0%

profile of v1, /device:TPU:10, one launch (start us, length us, event | category | flops | bytes accessed | tf_op | source)
XLA Modules:
  0.0 1052.7 jit_solution(4435498827576402804)
XLA Ops:
  12.7 1.9 bitcast_dynamic-update-slice_fusion.28
  29.2 1.9 bitcast_dynamic-update-slice_fusion.19
  40.1 1.9 bitcast_dynamic-update-slice_fusion.13
  42.0 1.9 bitcast_dynamic-update-slice_fusion.12
  43.9 1.9 bitcast_dynamic-update-slice_fusion.11
  49.4 1.8 bitcast_dynamic-update-slice_fusion.8
  58.5 1.8 bitcast_dynamic-update-slice_fusion.3
  65.9 6.1 all-to-all-start
  72.7 192.3 %all-gather.3.cloned.1.call-done = bf16[32,12,8192]{2,1,0:T(8,128)(2,1)} async-done(((bf16[1,12,8192]{2,1,0:T(8,128)(2,1)}), bf16[32,12,8192]{2,1,0:T(8,128)(2,1)}) %all-gather.3.cloned.1.call-update) | async-done | bytes 6291472 | tf_op jit(solution)/shard_map/all_gather | solution.py:34
  265.0 8.8 reshape.51
  273.7 4.2 convert_reduce_fusion
  279.0 147.9 %all-to-all-done = bf16[32,256,896]{2,1,0:T(8,128)(2,1)} async-done(((bf16[32,256,896]{2,1,0:T(8,128)(2,1)}), bf16[32,256,896]{2,1,0:T(8,128)(2,1)}, u32[]{:S(2)}, u32[]{:S(2)}) %all-to-all-start) | async-done | bytes 14680096 | tf_op jit(solution)/shard_map/all_to_all | solution.py:16
  426.9 12.0 %convolution_bitcast_fusion.1 = f32[384,896]{0,1:T(8,128)S(1)} fusion(bf16[8192,896]{1,0:T(8,128)(2,1)} %bitcast.38, bf16[384,8192]{1,0:T(8,128)(2,1)} %reshape.51), kind=kOutput, calls=%fused_computation.12 | convolution fusion | flops 5637144576 | bytes 22347776 | tf_op jit(solution)/shard_map/dot_general | solution.py:40
  440.5 16.6 %bitcast_convert_fusion = f32[8192,896]{1,0:T(8,128)} fusion(bf16[32,256,896]{2,1,0:T(8,128)(2,1)} %all-to-all-done), kind=kLoop, calls=%fused_computation.54 | loop fusion | flops 7340032 | bytes 44040192 | tf_op jit(solution)/shard_map/convert_element_type | solution.py:41
  457.0 541.8 %while.10 = (s32[]{:T(128)}, f32[4,896]{1,0:T(4,128)S(1)}, f32[4,8192]{1,0:T(4,128)S(1)}, f32[8192,896]{1,0:T(8,128)}, bf16[384,8192]{1,0:T(8,128)(2,1)}, /*index=5*/f32[384,896]{1,0:T(8,128)}, s32[]{:T(128)}, s32[]{:T(128)}) while((s32[]{:T(128)}, f32[4,896]{1,0:T(4,128)S(1)}, f32[4,8192]{1,0:T(4,128)S(1)}, f32[8192,896]{1,0:T(8,128)}, ...), condition=%wide.region_6.7_spmd, body=%wide.region_3.6_spmd.sunk | while | flops 5718973440 | bytes 214255232 | solution.py:53
  457.1 12.5 %abs_reduce_fusion.2 = f32[64,896]{1,0:T(8,128)S(1)} fusion(f32[64,128]{1,0:T(8,128)S(1)} %bitcast.108, f32[8192,896]{1,0:T(8,128)} %get-tuple-element.128), kind=kLoop, calls=%fused_computation.4.clone.1 | loop fusion | flops 21962752 | bytes 29622272 | tf_op jit(solution)/shard_map/while/body/eval_jaxpr/reduce_max | solution.py:46
  469.6 5.2 copy-done
  474.8 108.3 %fusion.20 = bf16[8192,896]{1,0:T(8,128)(2,1)S(1)} fusion(f32[8192,896]{1,0:T(8,128)S(1)} %copy-done, f32[64,896]{1,0:T(8,128)S(1)} %add_multiply_fusion.2, f32[8192]{0:T(1024)S(1)} %bitcast.109), kind=kLoop, calls=%fused_computation.3.clone.1 | loop fusion | flops 58720256 | bytes 44302336 | tf_op jit(solution)/shard_map/while/body/eval_jaxpr/convert_element_type | solution.py:48
  583.1 9.2 fusion.21
  592.5 12.5 %abs_reduce_fusion.2 = f32[64,896]{1,0:T(8,128)S(1)} fusion(f32[64,128]{1,0:T(8,128)S(1)} %bitcast.108, f32[8192,896]{1,0:T(8,128)} %get-tuple-element.128), kind=kLoop, calls=%fused_computation.4.clone.1 | loop fusion | flops 21962752 | bytes 29622272 | tf_op jit(solution)/shard_map/while/body/eval_jaxpr/reduce_max | solution.py:46
  605.0 5.2 copy-done
  610.3 108.3 %fusion.20 = bf16[8192,896]{1,0:T(8,128)(2,1)S(1)} fusion(f32[8192,896]{1,0:T(8,128)S(1)} %copy-done, f32[64,896]{1,0:T(8,128)S(1)} %add_multiply_fusion.2, f32[8192]{0:T(1024)S(1)} %bitcast.109), kind=kLoop, calls=%fused_computation.3.clone.1 | loop fusion | flops 58720256 | bytes 44302336 | tf_op jit(solution)/shard_map/while/body/eval_jaxpr/convert_element_type | solution.py:48
  718.6 9.3 fusion.21
  728.0 12.5 %abs_reduce_fusion.2 = f32[64,896]{1,0:T(8,128)S(1)} fusion(f32[64,128]{1,0:T(8,128)S(1)} %bitcast.108, f32[8192,896]{1,0:T(8,128)} %get-tuple-element.128), kind=kLoop, calls=%fused_computation.4.clone.1 | loop fusion | flops 21962752 | bytes 29622272 | tf_op jit(solution)/shard_map/while/body/eval_jaxpr/reduce_max | solution.py:46
  740.5 5.2 copy-done
  745.7 108.3 %fusion.20 = bf16[8192,896]{1,0:T(8,128)(2,1)S(1)} fusion(f32[8192,896]{1,0:T(8,128)S(1)} %copy-done, f32[64,896]{1,0:T(8,128)S(1)} %add_multiply_fusion.2, f32[8192]{0:T(1024)S(1)} %bitcast.109), kind=kLoop, calls=%fused_computation.3.clone.1 | loop fusion | flops 58720256 | bytes 44302336 | tf_op jit(solution)/shard_map/while/body/eval_jaxpr/convert_element_type | solution.py:48
  854.0 9.3 fusion.21
  863.4 12.5 %abs_reduce_fusion.2 = f32[64,896]{1,0:T(8,128)S(1)} fusion(f32[64,128]{1,0:T(8,128)S(1)} %bitcast.108, f32[8192,896]{1,0:T(8,128)} %get-tuple-element.128), kind=kLoop, calls=%fused_computation.4.clone.1 | loop fusion | flops 21962752 | bytes 29622272 | tf_op jit(solution)/shard_map/while/body/eval_jaxpr/reduce_max | solution.py:46
  875.9 5.2 copy-done
  881.2 108.3 %fusion.20 = bf16[8192,896]{1,0:T(8,128)(2,1)S(1)} fusion(f32[8192,896]{1,0:T(8,128)S(1)} %copy-done, f32[64,896]{1,0:T(8,128)S(1)} %add_multiply_fusion.2, f32[8192]{0:T(1024)S(1)} %bitcast.109), kind=kLoop, calls=%fused_computation.3.clone.1 | loop fusion | flops 58720256 | bytes 44302336 | tf_op jit(solution)/shard_map/while/body/eval_jaxpr/convert_element_type | solution.py:48
  989.5 9.3 fusion.21
  999.5 45.8 %psum.7 = f32[4]{0:T(128)S(1)} all-reduce(f32[4]{0:T(128)S(1)} %get-tuple-element.70), channel_id=1, replica_groups=mesh['dp'=32,'tensor'=1] {'dp','tensor'}, use_global_device_ids=true, to_apply=%region_8.9 | all-reduce | flops 4 | bytes 32 | tf_op jit(solution)/shard_map/psum | solution.py:54
  (57 shorter events, 50.7 us)
Async XLA Ops:
  65.9 361.0 %all-to-all-start = ((bf16[32,256,896]{2,1,0:T(8,128)(2,1)}), bf16[32,256,896]{2,1,0:T(8,128)(2,1)}, u32[]{:S(2)}, u32[]{:S(2)}) async-start(bf16[32,256,896]{2,1,0:T(8,128)(2,1)} %bitcast_dynamic-update-slice_fusion), calls=%async_computation | async-start | bytes 29360128 | tf_op jit(solution)/shard_map/all_to_all | solution.py:16
  71.9 193.0 %all-gather.3.cloned.1.call-start = ((), (), s32[]{:S(2)}) async-start(), calls=%async_computation.1 | async-start | bytes 8650752 | tf_op jit(solution)/shard_map/all_gather | solution.py:34
  457.1 17.8 %copy-start = (f32[8192,896]{1,0:T(8,128)S(1)}, f32[8192,896]{1,0:T(8,128)}, u32[]{:S(2)}) copy-start(f32[8192,896]{1,0:T(8,128)} %get-tuple-element.128) | copy-start | bytes 88080384 | tf_op jit(solution)/shard_map/while
  592.5 17.8 %copy-start = (f32[8192,896]{1,0:T(8,128)S(1)}, f32[8192,896]{1,0:T(8,128)}, u32[]{:S(2)}) copy-start(f32[8192,896]{1,0:T(8,128)} %get-tuple-element.128) | copy-start | bytes 88080384 | tf_op jit(solution)/shard_map/while
  728.0 17.8 %copy-start = (f32[8192,896]{1,0:T(8,128)S(1)}, f32[8192,896]{1,0:T(8,128)}, u32[]{:S(2)}) copy-start(f32[8192,896]{1,0:T(8,128)} %get-tuple-element.128) | copy-start | bytes 88080384 | tf_op jit(solution)/shard_map/while
  863.4 17.8 %copy-start = (f32[8192,896]{1,0:T(8,128)S(1)}, f32[8192,896]{1,0:T(8,128)}, u32[]{:S(2)}) copy-start(f32[8192,896]{1,0:T(8,128)} %get-tuple-element.128) | copy-start | bytes 88080384 | tf_op jit(solution)/shard_map/while
Sparse Core Ops, SparseCore 0:
  75.6 189.3 all-gather.2
